TPU v7x, 32 devices: a whole 2x2x4 slice. The times are simulated.
32 devices in a mesh: group: 4 (over y, x), fsdp: 2 (over core), tensor: 4 (over z).
Axes of the slice: x: 2, y: 2, z: 4, core: 2. Of those that a mesh axis runs over, the one named last changes fastest.
Arguments:
- patches: bfloat16 [4, 2, 8, 577, 1024], P('group', None, ('fsdp', 'tensor')), may hold values from -6 to 6
- output_grad: bfloat16 [4, 2, 8, 577, 1024], P('group', None, ('fsdp', 'tensor')), may hold values from -6 to 6
- live_counts: int32 [4, 2, 2], P('group'), may hold values from 1 to 4, as said below
- attn_master: float32 [4, 1024, 1024], P(None, 'fsdp', 'tensor')
- mlp_master: float32 [2, 1024, 4096], P(None, 'fsdp', 'tensor')
- vector_master: float32 [12, 1024], replicated
- attn_moments: float32 [4, 2, 4, 1024, 1024], P('group', None, None, 'fsdp', 'tensor'), as said below
- mlp_moments: float32 [4, 2, 2, 1024, 4096], P('group', None, None, 'fsdp', 'tensor'), as said below
- vector_moments: float32 [4, 2, 12, 1024], P('group'), as said below
- attn_outer: float32 [4, 1024, 1024], P(None, 'fsdp', 'tensor'), may hold values from -0.125 to 0.125
- mlp_outer: float32 [2, 1024, 4096], P(None, 'fsdp', 'tensor'), may hold values from -0.125 to 0.125
- vector_outer: float32 [12, 1024], replicated, may hold values from -0.625 to 0.625
Outputs:
- block_output: bfloat16 [4, 2, 8, 577, 1024], P('group', None, ('fsdp', 'tensor'))
- patches_grad: float32 [4, 2, 8, 577, 1024], P('group', None, ('fsdp', 'tensor'))
- attn_inner: float32 [4, 2, 4, 1024, 1024], P('group', None, None, 'fsdp', 'tensor')
- attn_state: float32 [3, 4, 1024, 1024], P(None, None, 'fsdp', 'tensor')
- attn_copy: bfloat16 [4, 1024, 1024], P(None, 'fsdp', 'tensor')
- mlp_inner: float32 [4, 2, 2, 1024, 4096], P('group', None, None, 'fsdp', 'tensor')
- mlp_state: float32 [3, 2, 1024, 4096], P(None, None, 'fsdp', 'tensor')
- mlp_copy: bfloat16 [2, 1024, 4096], P(None, 'fsdp', 'tensor')
- vector_inner: float32 [4, 2, 12, 1024], P('group')
- vector_state: float32 [3, 12, 1024], replicated
- vector_copy: bfloat16 [12, 1024], replicated
Inputs may be any that keep to these rules, and one draw needn't show every extreme that they name: live_counts[g, m, f] images are live, and they stand first, among the f-th block of 4 image slots of micro-batch m in group g; some entry equals 4. `attn_moments`: second moments are positive. `mlp_moments`: second moments are positive. `vector_moments`: second moments are positive.
All inputs are finite; a program needn't handle non-finite values.
Results may differ from a plain program's by a relative error of at most 0.012.
The roundings to bfloat16 on the way count: a program that leaves them out, or rounds other values in their place, can miss the bound.
Values may be sent and summed in bfloat16 or wider, within the bound.
A program may use at most 320 MiB of HBM per device.

v0:
```python
from functools import partial

import jax
import jax.numpy as jnp
from jax import lax
from jax.sharding import PartitionSpec as P

HD = 64
FF = 4096
STEP = 8


EPSILON = 1e-06
INNER_RATE = 0.02
VECTOR_RATE = 0.2
WEIGHT_DECAY = 0.1
OUTER_RATE = 0.7
OUTER_MOMENTUM = 0.9


def normalize(source, gain_row, shift_row):
    centre = source - jnp.mean(source, axis=-1, keepdims=True)
    spread = jnp.mean(centre * centre, axis=-1, keepdims=True)
    return centre * lax.rsqrt(spread + EPSILON) * gain_row + shift_row


def gelu_exact(source):
    return jax.nn.gelu(source, approximate=False)


def gelu_slope(source):
    return (
        0.5 * (1.0 + lax.erf(source * 0.7071067811865476))
        + source * jnp.exp(-0.5 * source * source) * 0.3989422804014327
    )


def inner_adamw(master, gradient, moments, step_rate, decay_rate):
    first_moment = 0.9 * moments[0] + 0.1 * gradient
    second_moment = 0.95 * moments[1] + 0.05 * gradient * gradient
    step_ratio = (
        first_moment / (1.0 - 0.9**STEP) / (jnp.sqrt(second_moment / (1.0 - 0.95**STEP)) + 1e-08)
    )
    return (master - step_rate * (step_ratio + decay_rate * master), second_moment)


def outer_nesterov(master, outer_old, difference):
    momentum = OUTER_MOMENTUM * outer_old + difference
    updated = master - OUTER_RATE * (difference + OUTER_MOMENTUM * momentum)
    return (jnp.stack([difference, momentum, updated]), updated.astype(jnp.bfloat16))


def attend_forward(score_scale, operands):
    queries_low, keys_low, values_low = operands
    scores = (
        jnp.einsum("qhe,khe->hqk", queries_low, keys_low, preferred_element_type=jnp.float32)
        * score_scale
    )
    highest = jnp.max(scores, axis=-1, keepdims=True)
    exponent = jnp.exp(scores - highest)
    totals = jnp.sum(exponent, axis=-1, keepdims=True)
    probs_low = (exponent / totals).astype(jnp.bfloat16)
    attended = jnp.einsum("hqk,khe->qhe", probs_low, values_low, preferred_element_type=jnp.float32)
    return (attended.astype(jnp.bfloat16), (highest + jnp.log(totals))[..., 0])


def attend_backward(score_scale, operands):
    queries_low, keys_low, values_low, log_totals, grad_attended = operands
    scores = (
        jnp.einsum("qhe,khe->hqk", queries_low, keys_low, preferred_element_type=jnp.float32)
        * score_scale
    )
    probs_full = jnp.exp(scores - log_totals[..., None])
    grad_probs = jnp.einsum(
        "qhe,khe->hqk", grad_attended, values_low, preferred_element_type=jnp.float32
    )
    grad_values = jnp.einsum(
        "hqk,qhe->khe",
        probs_full.astype(jnp.bfloat16),
        grad_attended,
        preferred_element_type=jnp.float32,
    )
    weighted = jnp.sum(probs_full * grad_probs, axis=-1, keepdims=True)
    grad_scores = (probs_full * (grad_probs - weighted)).astype(jnp.bfloat16)
    grad_queries = (
        jnp.einsum("hqk,khe->qhe", grad_scores, keys_low, preferred_element_type=jnp.float32)
        * score_scale
    )
    grad_keys = (
        jnp.einsum("hqk,qhe->khe", grad_scores, queries_low, preferred_element_type=jnp.float32)
        * score_scale
    )
    return (
        grad_queries.astype(jnp.bfloat16),
        grad_keys.astype(jnp.bfloat16),
        grad_values.astype(jnp.bfloat16),
    )


def local(
    patches,
    output_grad,
    live_counts,
    attn_master,
    mlp_master,
    vector_master,
    attn_moments,
    mlp_moments,
    vector_moments,
    attn_outer,
    mlp_outer,
    vector_outer,
):
    narrow = jnp.bfloat16
    single = jnp.float32
    tensor_index = lax.axis_index("tensor")
    fsdp_index = lax.axis_index("fsdp")
    micro_count = patches.shape[1]
    local_images = patches.shape[2]
    seq_len = patches.shape[3]
    width = patches.shape[4]
    head_cols = attn_master.shape[2]
    hidden_cols = mlp_master.shape[2]
    score_scale = HD ** (-0.5)
    attn_all, mlp_all = (
        lax.all_gather(attn_master.astype(narrow), "fsdp", axis=1, tiled=True),
        lax.all_gather(mlp_master.astype(narrow), "fsdp", axis=1, tiled=True),
    )
    bias_query = lax.dynamic_slice_in_dim(vector_master[4], tensor_index * head_cols, head_cols)
    bias_value = lax.dynamic_slice_in_dim(vector_master[5], tensor_index * head_cols, head_cols)
    head_width = attn_all.shape[2]
    heads_here = head_width // HD
    bias_hidden = lax.dynamic_slice_in_dim(
        vector_master[8:].reshape(-1), tensor_index * hidden_cols, hidden_cols
    )
    owner_counts = jnp.sum(
        jnp.where(jnp.arange(live_counts.shape[2]) == fsdp_index, live_counts[0], 0), axis=-1
    )
    slot_index = tensor_index * local_images + jnp.arange(local_images)
    alive_all = (slot_index[None, :] < owner_counts[:, None]).astype(single)
    forward_attend = partial(attend_forward, score_scale)
    backward_attend = partial(attend_backward, score_scale)
    qkv_acc = jnp.zeros((3, width, head_width), single)
    out_acc = jnp.zeros((width, head_width), single)
    fc_in_acc = jnp.zeros((width, hidden_cols), single)
    fc_out_acc = jnp.zeros((width, hidden_cols), single)
    hidden_bias_acc = jnp.zeros((hidden_cols,), single)
    query_bias_acc = jnp.zeros((head_width,), single)
    value_bias_acc = jnp.zeros((head_width,), single)
    vector_acc = jnp.zeros((6, width), single)
    outputs_mixed = []
    outputs_grad = []
    for batch_index in range(micro_count):
        inputs = patches[0, batch_index].astype(single)
        alive = alive_all[batch_index][:, None, None]
        normed_one = normalize(inputs, vector_master[0], vector_master[1]).astype(narrow)
        rows_attn = lax.all_gather(normed_one, "tensor", axis=0, tiled=True)
        image_count = rows_attn.shape[0]
        shape_heads = (image_count, seq_len, heads_here, HD)
        projected = jnp.einsum(
            "isd,jde->jise", rows_attn, attn_all[:3], preferred_element_type=single
        )
        queries_low = (projected[0] + bias_query).astype(narrow).reshape(shape_heads)
        keys_low = projected[1].astype(narrow).reshape(shape_heads)
        values_low = (projected[2] + bias_value).astype(narrow).reshape(shape_heads)
        attended, log_totals = lax.map(forward_attend, (queries_low, keys_low, values_low))
        attended = attended.reshape(image_count, seq_len, head_width)
        branch_one = lax.psum_scatter(
            jnp.einsum("ise,de->isd", attended, attn_all[3], preferred_element_type=single),
            "tensor",
            scatter_dimension=0,
            tiled=True,
        )
        resid_one = inputs + branch_one + vector_master[6]
        normed_two = normalize(resid_one, vector_master[2], vector_master[3]).astype(narrow)
        rows_mlp = lax.all_gather(normed_two, "tensor", axis=0, tiled=True)
        pre_act = (
            jnp.einsum("isd,df->isf", rows_mlp, mlp_all[0], preferred_element_type=single)
            + bias_hidden
        )
        hidden = gelu_exact(pre_act).astype(narrow)
        branch_two = lax.psum_scatter(
            jnp.einsum("isf,df->isd", hidden, mlp_all[1], preferred_element_type=single),
            "tensor",
            scatter_dimension=0,
            tiled=True,
        )
        outputs_mixed.append((alive * (resid_one + branch_two + vector_master[7])).astype(narrow))
        grad_out = alive * output_grad[0, batch_index].astype(single)
        rows_grad_two = lax.all_gather(grad_out.astype(narrow), "tensor", axis=0, tiled=True)
        fc_out_acc = fc_out_acc + jnp.einsum(
            "isd,isf->df", rows_grad_two, hidden, preferred_element_type=single
        )
        grad_hidden = jnp.einsum(
            "isd,df->isf", rows_grad_two, mlp_all[1], preferred_element_type=single
        )
        grad_pre = (grad_hidden * gelu_slope(pre_act)).astype(narrow)
        fc_in_acc = fc_in_acc + jnp.einsum(
            "isd,isf->df", rows_mlp, grad_pre, preferred_element_type=single
        )
        hidden_bias_acc = hidden_bias_acc + jnp.sum(grad_pre.astype(single), axis=(0, 1))
        grad_normed_two = lax.psum_scatter(
            jnp.einsum("isf,df->isd", grad_pre, mlp_all[0], preferred_element_type=single),
            "tensor",
            scatter_dimension=0,
            tiled=True,
        )
        unused_two, norm_pull_two = jax.vjp(
            normalize, resid_one, vector_master[2], vector_master[3]
        )
        back_resid, gain_two, shift_two = norm_pull_two(grad_normed_two)
        grad_resid = grad_out + back_resid
        rows_grad_one = lax.all_gather(grad_resid.astype(narrow), "tensor", axis=0, tiled=True)
        out_acc = out_acc + jnp.einsum(
            "isd,ise->de", rows_grad_one, attended, preferred_element_type=single
        )
        grad_attended = jnp.einsum(
            "isd,de->ise", rows_grad_one, attn_all[3], preferred_element_type=single
        ).astype(narrow)
        grad_queries, grad_keys, grad_values = lax.map(
            backward_attend,
            (queries_low, keys_low, values_low, log_totals, grad_attended.reshape(shape_heads)),
        )
        grad_queries = grad_queries.reshape(image_count, seq_len, head_width)
        grad_keys = grad_keys.reshape(image_count, seq_len, head_width)
        grad_values = grad_values.reshape(image_count, seq_len, head_width)
        grad_stack = jnp.stack([grad_queries, grad_keys, grad_values])
        qkv_acc = qkv_acc + jnp.einsum(
            "isd,jise->jde", rows_attn, grad_stack, preferred_element_type=single
        )
        query_bias_acc = query_bias_acc + jnp.sum(grad_queries.astype(single), axis=(0, 1))
        value_bias_acc = value_bias_acc + jnp.sum(grad_values.astype(single), axis=(0, 1))
        summed = jnp.einsum("ise,de->isd", grad_queries, attn_all[0], preferred_element_type=single)
        summed = summed + jnp.einsum(
            "ise,de->isd", grad_keys, attn_all[1], preferred_element_type=single
        )
        grad_normed_one = lax.psum_scatter(
            summed
            + jnp.einsum("ise,de->isd", grad_values, attn_all[2], preferred_element_type=single),
            "tensor",
            scatter_dimension=0,
            tiled=True,
        )
        unused_one, norm_pull_one = jax.vjp(normalize, inputs, vector_master[0], vector_master[1])
        back_inputs, gain_one, shift_one = norm_pull_one(grad_normed_one)
        outputs_grad.append(grad_resid + back_inputs)
        vector_acc = vector_acc + jnp.stack(
            [
                gain_one,
                shift_one,
                gain_two,
                shift_two,
                jnp.sum(grad_resid, axis=(0, 1)),
                jnp.sum(grad_out, axis=(0, 1)),
            ]
        )
    attn_grad_full = jnp.concatenate([qkv_acc, out_acc[None]], 0)
    query_row = lax.dynamic_update_slice_in_dim(
        jnp.zeros((width,), single), query_bias_acc, tensor_index * head_cols, 0
    )
    value_row = lax.dynamic_update_slice_in_dim(
        jnp.zeros((width,), single), value_bias_acc, tensor_index * head_cols, 0
    )
    mlp_grad_cols = jnp.stack([fc_in_acc, fc_out_acc])
    attn_grad, mlp_grad = (
        lax.psum_scatter(attn_grad_full, "fsdp", scatter_dimension=1, tiled=True),
        lax.psum_scatter(mlp_grad_cols, "fsdp", scatter_dimension=1, tiled=True),
    )
    hidden_rows = lax.dynamic_update_slice_in_dim(
        jnp.zeros((FF,), single), hidden_bias_acc, tensor_index * hidden_cols, 0
    ).reshape(-1, width)
    vector_part = jnp.concatenate(
        [vector_acc[:4], jnp.stack([query_row, value_row]), vector_acc[4:], hidden_rows], 0
    )
    vector_grad = lax.psum(vector_part, ("fsdp", "tensor"))
    new_attn, second_attn = inner_adamw(
        attn_master, attn_grad, attn_moments[0], INNER_RATE, WEIGHT_DECAY
    )
    new_mlp, second_mlp = inner_adamw(
        mlp_master, mlp_grad, mlp_moments[0], INNER_RATE, WEIGHT_DECAY
    )
    new_vector, second_vector = inner_adamw(
        vector_master, vector_grad, vector_moments[0], VECTOR_RATE, 0.0
    )
    diff_attn, diff_mlp, diff_vector = lax.psum(
        (attn_master - new_attn, mlp_master - new_mlp, vector_master - new_vector), "group"
    )
    groups = lax.axis_size("group")
    attn_state, attn_copy = outer_nesterov(attn_master, attn_outer, diff_attn / groups)
    mlp_state, mlp_copy = outer_nesterov(mlp_master, mlp_outer, diff_mlp / groups)
    vector_state, vector_copy = outer_nesterov(vector_master, vector_outer, diff_vector / groups)
    block_output = jnp.stack(outputs_mixed)[None]
    patches_grad = jnp.stack(outputs_grad)[None]
    attn_inner = jnp.stack([attn_grad, second_attn])[None]
    mlp_inner = jnp.stack([mlp_grad, second_mlp])[None]
    vector_inner = jnp.stack([vector_grad, second_vector])[None]
    return (
        block_output,
        patches_grad,
        attn_inner,
        attn_state,
        attn_copy,
        mlp_inner,
        mlp_state,
        mlp_copy,
        vector_inner,
        vector_state,
        vector_copy,
    )


def solution(mesh):
    placed = (
        P("group", None, ("fsdp", "tensor"), None, None),
        P("group", None, ("fsdp", "tensor"), None, None),
        P("group", None, None),
        P(None, "fsdp", "tensor"),
        P(None, "fsdp", "tensor"),
        P(),
        P("group", None, None, "fsdp", "tensor"),
        P("group", None, None, "fsdp", "tensor"),
        P("group", None, None, None),
        P(None, "fsdp", "tensor"),
        P(None, "fsdp", "tensor"),
        P(),
    )
    return jax.shard_map(
        local,
        mesh=mesh,
        in_specs=placed,
        out_specs=(
            P("group", None, ("fsdp", "tensor"), None, None),
            P("group", None, ("fsdp", "tensor"), None, None),
            P("group", None, None, "fsdp", "tensor"),
            P(None, None, "fsdp", "tensor"),
            P(None, "fsdp", "tensor"),
            P("group", None, None, "fsdp", "tensor"),
            P(None, None, "fsdp", "tensor"),
            P(None, "fsdp", "tensor"),
            P("group", None, None, None),
            P(),
            P(),
        ),
        check_vma=False,
    )
```

profile of v0, /device:TPU:0, one launch (start us, length us, event | category | flops | bytes accessed | tf_op | source)
XLA Modules:
  0.0 2520.2 jit_solution(1555532051777853854)
XLA Ops:
  23.5 93.8 %all-gather.19.cloned.1.call-done = bf16[4,577,1024]{2,1,0:T(8,128)(2,1)} async-done(((bf16[1,577,1024]{2,1,0:T(8,128)(2,1)}), bf16[4,577,1024]{2,1,0:T(8,128)(2,1)}) %all-gather.19.cloned.1.call-update) | async-done | bytes 4726800 | tf_op jit(solution)/shard_map/all_gather | solution.py:157
  126.6 81.8 %all-gather.11.cloned.1.call-done = bf16[4,577,1024]{2,1,0:T(8,128)(2,1)} async-done(((bf16[1,577,1024]{2,1,0:T(8,128)(2,1)}), bf16[4,577,1024]{2,1,0:T(8,128)(2,1)}) %all-gather.11.cloned.1.call-update) | async-done | bytes 4726800 | tf_op jit(solution)/shard_map/all_gather | solution.py:157
  240.4 25.3 %while.53 = (s32[]{:T(128)}, bf16[4,577,4,64]{1,3,2,0:T(8,128)(2,1)}, f32[4,4,577]{2,1,0:T(4,128)S(1)}, bf16[4,577,4,64]{1,3,2,0:T(8,128)(2,1)}, bf16[4,577,4,64...) while((s32[]{:T(128)}, bf16[4,577,4,64]{1,3,2,0:T(8,128)(2,1)}, ...), condition=%wide.region_16.17_spmd, body=%wide.region_13.16_spmd.sunk | while | flops 353050112 | bytes 17370320 | solution.py:166
  289.0 21.4 while.52
  322.3 112.6 %reduce-scatter.15.cloned.1.call-done = f32[1,577,1024]{2,1,0:T(8,128)} async-done(((f32[4,577,1024]{2,1,0:T(8,128)}), f32[1,577,1024]{2,1,0:T(8,128)}) %reduce-scatter.15.cloned.1.call-update) | async-done | bytes 2363408 | tf_op jit(solution)/shard_map/reduce_scatter | solution.py:168
  434.9 167.1 %reduce-scatter.11.cloned.1.call-done = f32[1,577,1024]{2,1,0:T(8,128)} async-done(((f32[4,577,1024]{2,1,0:T(8,128)}), f32[1,577,1024]{2,1,0:T(8,128)}) %reduce-scatter.11.cloned.1.call-update) | async-done | bytes 2363408 | tf_op jit(solution)/shard_map/reduce_scatter | solution.py:168
  629.0 83.5 %all-gather.21.cloned.1.call-done = bf16[4,577,1024]{2,1,0:T(8,128)(2,1)} async-done(((bf16[1,577,1024]{2,1,0:T(8,128)(2,1)}), bf16[4,577,1024]{2,1,0:T(8,128)(2,1)}) %all-gather.21.cloned.1.call-update) | async-done | bytes 4726800 | tf_op jit(solution)/shard_map/all_gather | solution.py:176
  722.7 80.8 %all-gather.15.cloned.1.call-done = bf16[4,577,1024]{2,1,0:T(8,128)(2,1)} async-done(((bf16[1,577,1024]{2,1,0:T(8,128)(2,1)}), bf16[4,577,1024]{2,1,0:T(8,128)(2,1)}) %all-gather.15.cloned.1.call-update) | async-done | bytes 4726800 | tf_op jit(solution)/shard_map/all_gather | solution.py:176
  803.5 20.2 fusion.210
  823.8 70.2 %all-gather.23.cloned.1.call-done = bf16[4,577,1024]{2,1,0:T(8,128)(2,1)} async-done(((bf16[1,577,1024]{2,1,0:T(8,128)(2,1)}), bf16[4,577,1024]{2,1,0:T(8,128)(2,1)}) %all-gather.23.cloned.1.call-update) | async-done | bytes 4726800 | tf_op jit(solution)/shard_map/all_gather | solution.py:190
  916.6 67.7 %all-gather.27.cloned.1.call-done = bf16[4,577,1024]{2,1,0:T(8,128)(2,1)} async-done(((bf16[1,577,1024]{2,1,0:T(8,128)(2,1)}), bf16[4,577,1024]{2,1,0:T(8,128)(2,1)}) %all-gather.27.cloned.1.call-update) | async-done | bytes 4726800 | tf_op jit(solution)/shard_map/all_gather | solution.py:190
  1006.7 46.7 %fusion.116 = (bf16[4,577,1024]{2,1,0:T(8,128)(2,1)S(1)}, bf16[4,577,1024]{2,1,0:T(8,128)(2,1)}) fusion(f32[4,577,1024]{2,1,0:T(8,128)} %get-tuple-element.421, f32[1024]{0:T(1024)S(1)} %dynamic_slice.61, u8[577,1024]{1,0:T(8,128)(4,1)} %get-tuple-element.249, u8[577,1024]{1,0:T(8,128)(4,1)S(1)} %get-tuple-element.248, ...), kind=kLoop, calls=%fused_computation.127 | loop fusion | flops 333238272 | bytes 30728192 | tf_op jit(solution)/shard_map/convert_element_type | solution.py:181
  1074.1 74.3 %reduce-scatter.19.cloned.1.call-done = f32[1,577,1024]{2,1,0:T(8,128)} async-done(((f32[4,577,1024]{2,1,0:T(8,128)}), f32[1,577,1024]{2,1,0:T(8,128)}) %reduce-scatter.19.cloned.1.call-update) | async-done | bytes 2363408 | tf_op jit(solution)/shard_map/reduce_scatter | solution.py:202
  1148.4 166.5 %reduce-scatter.23.cloned.1.call-done = f32[1,577,1024]{2,1,0:T(8,128)} async-done(((f32[4,577,1024]{2,1,0:T(8,128)}), f32[1,577,1024]{2,1,0:T(8,128)}) %reduce-scatter.23.cloned.1.call-update) | async-done | bytes 2363408 | tf_op jit(solution)/shard_map/reduce_scatter | solution.py:202
  1320.2 161.4 %reduce-scatter.13.cloned.1.call-done = f32[1,577,1024]{2,1,0:T(8,128)} async-done(((f32[4,577,1024]{2,1,0:T(8,128)}), f32[1,577,1024]{2,1,0:T(8,128)}) %reduce-scatter.13.cloned.1.call-update) | async-done | bytes 2363408 | tf_op jit(solution)/shard_map/reduce_scatter | solution.py:182
  1481.5 167.1 %reduce-scatter.17.cloned.1.call-done = f32[1,577,1024]{2,1,0:T(8,128)} async-done(((f32[4,577,1024]{2,1,0:T(8,128)}), f32[1,577,1024]{2,1,0:T(8,128)}) %reduce-scatter.17.cloned.1.call-update) | async-done | bytes 2363408 | tf_op jit(solution)/shard_map/reduce_scatter | solution.py:182
  1700.1 51.5 %all-gather.29.cloned.1.call-done = bf16[4,577,1024]{2,1,0:T(8,128)(2,1)} async-done(((bf16[1,577,1024]{2,1,0:T(8,128)(2,1)}), bf16[4,577,1024]{2,1,0:T(8,128)(2,1)}) %all-gather.29.cloned.1.call-update) | async-done | bytes 4726800 | tf_op jit(solution)/shard_map/all_gather | solution.py:213
  1759.6 48.8 %while.55 = (s32[]{:T(128)}, bf16[4,577,4,64]{1,3,2,0:T(8,128)(2,1)S(1)}, bf16[4,577,4,64]{1,3,2,0:T(8,128)(2,1)}, bf16[4,577,4,64]{1,3,2,0:T(8,128)(2,1)}, bf16...) while((s32[]{:T(128)}, ...), condition=%wide.region_35.36_spmd, body=%wide.region_33.35_spmd.sunk | while | flops 869015040 | bytes 49660196 | solution.py:220
  1808.3 34.1 %all-gather.25.cloned.1.call-done = bf16[4,577,1024]{2,1,0:T(8,128)(2,1)} async-done(((bf16[1,577,1024]{2,1,0:T(8,128)(2,1)}), bf16[4,577,1024]{2,1,0:T(8,128)(2,1)}) %all-gather.25.cloned.1.call-update) | async-done | bytes 4726800 | tf_op jit(solution)/shard_map/all_gather | solution.py:213
  1858.2 53.2 %while.54 = (s32[]{:T(128)}, bf16[4,577,4,64]{1,3,2,0:T(8,128)(2,1)S(1)}, bf16[4,577,4,64]{1,3,2,0:T(8,128)(2,1)}, bf16[4,577,4,64]{1,3,2,0:T(8,128)(2,1)}, bf16...) while((s32[]{:T(128)}, ...), condition=%wide.region_26.27_spmd, body=%wide.region_24.26_spmd.sunk | while | flops 869015040 | bytes 49660196 | solution.py:220
  2025.0 79.5 %all-reduce.3.cloned.1.call-done = (f32[4,512,256]{1,2,0:T(8,128)}, f32[2,512,1024]{2,1,0:T(8,128)}) async-done(((f32[4,512,256]{1,2,0:T(8,128)}, f32[2,512,1024]{2,1,0:T(8,128)}), (f32[4,512,256]{1,2,0:T(8,128)}, f32[2,512,1024]{2,1,0:T(8,128)})) %all-reduce.3.cloned.1.call-update) | async-done | bytes 6291472 | tf_op jit(solution)/shard_map/psum | solution.py:285
  2145.1 124.9 %reduce-scatter.21.cloned.1.call-done = f32[1,577,1024]{2,1,0:T(8,128)} async-done(((f32[4,577,1024]{2,1,0:T(8,128)}), f32[1,577,1024]{2,1,0:T(8,128)}) %reduce-scatter.21.cloned.1.call-update) | async-done | bytes 2363408 | tf_op jit(solution)/shard_map/reduce_scatter | solution.py:237
  2272.4 164.3 %reduce-scatter.25.cloned.1.call-done = f32[1,577,1024]{2,1,0:T(8,128)} async-done(((f32[4,577,1024]{2,1,0:T(8,128)}), f32[1,577,1024]{2,1,0:T(8,128)}) %reduce-scatter.25.cloned.1.call-update) | async-done | bytes 2363408 | tf_op jit(solution)/shard_map/reduce_scatter | solution.py:237
  2447.5 29.4 %psum.30 = f32[12,1024]{1,0:T(8,128)S(1)} all-reduce(f32[12,1024]{1,0:T(8,128)S(1)} %concatenate.7), channel_id=1, replica_groups=mesh['group'=4,'fsdp'=2,'tensor'=4] {'fsdp','tensor'}, use_global_device_ids=true, to_apply=%region_61.62 | all-reduce | flops 12288 | bytes 98304 | tf_op jit(solution)/shard_map/psum | solution.py:275
  (490 shorter events, 626.4 us)
Async XLA Ops:
  7.2 16.3 all-gather.13.cloned.1.call-start
  10.1 107.3 %all-gather.19.cloned.1.call-start = ((), (), s32[]{:S(2)}) async-start(), calls=%async_computation.16 | async-start | bytes 5980160 | tf_op jit(solution)/shard_map/all_gather | solution.py:157
  19.3 189.1 %all-gather.11.cloned.1.call-start = ((), (), s32[]{:S(2)}) async-start(), calls=%async_computation.10 | async-start | bytes 5980160 | tf_op jit(solution)/shard_map/all_gather | solution.py:157
  20.0 414.9 %reduce-scatter.15.cloned.1.call-start = ((), (), s32[]{:S(2)}) async-start(), calls=%async_computation.17 | async-start | bytes 11960320 | tf_op jit(solution)/shard_map/reduce_scatter | solution.py:168
  273.1 328.9 %reduce-scatter.11.cloned.1.call-start = ((), (), s32[]{:S(2)}) async-start(), calls=%async_computation.12 | async-start | bytes 11960320 | tf_op jit(solution)/shard_map/reduce_scatter | solution.py:168
  318.4 310.6 %all-gather.17.cloned.1.call-start = ((), (), s32[]{:S(2)}) async-start(), calls=%async_computation.14 | async-start | bytes 6291456 | tf_op jit(solution)/shard_map/all_gather | solution.py:127
  322.3 390.2 %all-gather.21.cloned.1.call-start = ((), (), s32[]{:S(2)}) async-start(), calls=%async_computation.18 | async-start | bytes 5980160 | tf_op jit(solution)/shard_map/all_gather | solution.py:176
  608.9 194.7 %all-gather.15.cloned.1.call-start = ((), (), s32[]{:S(2)}) async-start(), calls=%async_computation.13 | async-start | bytes 5980160 | tf_op jit(solution)/shard_map/all_gather | solution.py:176
  609.6 284.4 %all-gather.23.cloned.1.call-start = ((), (), s32[]{:S(2)}) async-start(), calls=%async_computation.20 | async-start | bytes 5980160 | tf_op jit(solution)/shard_map/all_gather | solution.py:190
  623.3 361.0 %all-gather.27.cloned.1.call-start = ((), (), s32[]{:S(2)}) async-start(), calls=%async_computation.24 | async-start | bytes 5980160 | tf_op jit(solution)/shard_map/all_gather | solution.py:190
  627.9 520.5 %reduce-scatter.19.cloned.1.call-start = ((), (), s32[]{:S(2)}) async-start(), calls=%async_computation.21 | async-start | bytes 11960320 | tf_op jit(solution)/shard_map/reduce_scatter | solution.py:202
  916.6 398.3 %reduce-scatter.23.cloned.1.call-start = ((), (), s32[]{:S(2)}) async-start(), calls=%async_computation.25 | async-start | bytes 11960320 | tf_op jit(solution)/shard_map/reduce_scatter | solution.py:202
  1006.6 474.9 %reduce-scatter.13.cloned.1.call-start = ((), (), s32[]{:S(2)}) async-start(), calls=%async_computation.15 | async-start | bytes 11960320 | tf_op jit(solution)/shard_map/reduce_scatter | solution.py:182
  1063.4 585.3 %reduce-scatter.17.cloned.1.call-start = ((), (), s32[]{:S(2)}) async-start(), calls=%async_computation.19 | async-start | bytes 11960320 | tf_op jit(solution)/shard_map/reduce_scatter | solution.py:182
  1074.0 574.6 %copy-start.63 = (f32[1,1024]{1,0:T(1,128)S(1)}, f32[1,1024]{1,0:T(1,128)}, u32[]{:S(2)}) copy-start(f32[1,1024]{1,0:T(1,128)} %get-tuple-element.390) | copy-start | bytes 12292
  1074.0 677.5 %all-gather.29.cloned.1.call-start = ((), (), s32[]{:S(2)}) async-start(), calls=%async_computation.26 | async-start | bytes 5980160 | tf_op jit(solution)/shard_map/all_gather | solution.py:213
  1659.9 182.5 %all-gather.25.cloned.1.call-start = ((), (), s32[]{:S(2)}) async-start(), calls=%async_computation.22 | async-start | bytes 5980160 | tf_op jit(solution)/shard_map/all_gather | solution.py:213
  1664.5 286.9 %reduce-scatter.29.cloned.1.call-start = ((), (), s32[]{:S(2)}) async-start(), calls=%async_computation.29 | async-start | bytes 12582912 | tf_op jit(solution)/shard_map/reduce_scatter | solution.py:267
  1699.8 261.0 %reduce-scatter.27.cloned.1.call-start = ((), (), s32[]{:S(2)}) async-start(), calls=%async_computation.28 | async-start | bytes 6291456 | tf_op jit(solution)/shard_map/reduce_scatter | solution.py:266
  1936.8 167.7 %all-reduce.3.cloned.1.call-start = ((), (), s32[]{:S(2)}) async-start(), calls=%async_computation.30 | async-start | bytes 12582912 | tf_op jit(solution)/shard_map/psum | solution.py:285
  1968.0 302.0 %reduce-scatter.21.cloned.1.call-start = ((), (), s32[]{:S(2)}) async-start(), calls=%async_computation.23 | async-start | bytes 11960320 | tf_op jit(solution)/shard_map/reduce_scatter | solution.py:237
  1981.2 455.5 %reduce-scatter.25.cloned.1.call-start = ((), (), s32[]{:S(2)}) async-start(), calls=%async_computation.27 | async-start | bytes 11960320 | tf_op jit(solution)/shard_map/reduce_scatter | solution.py:237
  2145.1 291.6 %copy-start.39 = (f32[577]{0:T(1024)S(1)}, f32[577]{0:T(1024)}, u32[]{:S(2)}) copy-start(f32[577]{0:T(1024)} %copy-done.38) | copy-start | bytes 6928
  2145.1 291.6 %copy-start.49 = (f32[577]{0:T(1024)S(1)}, f32[577]{0:T(1024)}, u32[]{:S(2)}) copy-start(f32[577]{0:T(1024)} %copy-done.48) | copy-start | bytes 6928
  (94 other events, 2272.6 us)
Sparse Core Ops, SparseCore 0:
  10.2 13.2 all-gather.12
  25.7 91.6 all-gather.18
  119.5 88.8 all-gather.10
  273.2 161.6 reduce-scatter.14
  437.7 164.2 reduce-scatter.10
  603.9 14.6 all-gather.16
  620.8 91.6 all-gather.20
  714.6 88.8 all-gather.14
  805.1 88.8 all-gather.22
  895.4 88.8 all-gather.26
  986.7 161.6 reduce-scatter.18
  1150.6 164.2 reduce-scatter.22
  1317.2 164.2 reduce-scatter.12
  1484.3 164.2 reduce-scatter.16
  1660.0 91.4 all-gather.28
  1753.6 88.8 all-gather.24
  1845.2 14.7 reduce-scatter.28
  1937.0 10.1 reduce-scatter.26
  1968.1 136.3 all-reduce.2
  2106.7 163.2 reduce-scatter.20
  2272.4 164.2 reduce-scatter.24
where the time goes:
time: 2530 us; the launch traced here: 2520 us
  waiting for transfers between devices  1790 us (71%)
  matrix products  322 us (13%)
  other arithmetic  213 us (8%)
  local copies, waits for them, and re-layouts  124 us (5%)
  blocking collectives  46.9 us (2%)
    reduce_scatter x2, waiting for transfers between devices, local(): lax.psum_scatter(jnp.einsum('isf,df->isd', hidden, mlp_all[1], preferred_...  328 us
    reduce_scatter x2, waiting for transfers between devices, local(): lax.psum_scatter(summed + jnp.einsum('ise,de->isd', grad_values, attn_all...  289 us
    reduce_scatter x2, waiting for transfers between devices, local(): lax.psum_scatter(jnp.einsum('ise,de->isd', attended, attn_all[3], preferr...  280 us
    reduce_scatter x2, waiting for transfers between devices, local(): lax.psum_scatter(jnp.einsum('isf,df->isd', grad_pre, mlp_all[0], preferre...  241 us
    all_gather x2, waiting for transfers between devices, local(): rows_attn = lax.all_gather(normed_one, 'tensor', axis=0, tiled=True)  176 us
    all_gather x2, waiting for transfers between devices, local(): rows_mlp = lax.all_gather(normed_two, 'tensor', axis=0, tiled=True)  164 us
    all_gather x2, waiting for transfers between devices, local(): lax.all_gather(grad_out.astype(narrow), 'tensor', axis=0, tiled=True)  138 us
    all_gather x2, waiting for transfers between devices, local(): lax.all_gather(grad_resid.astype(narrow), 'tensor', axis=0, tiled=True)  85.6 us
  transfers between devices with their start and end apart: 21, of which 18 were waited for; matrix products, arithmetic and copies ran while one was open for 21% of the time, Pallas kernels for 0%

commit v1 on v0

v1 whole, which is shorter than its diff:
```python
from functools import partial

import jax
import jax.numpy as jnp
from jax import lax
from jax.sharding import PartitionSpec as P

HD = 64
FF = 4096
STEP = 8


EPSILON = 1e-06
INNER_RATE = 0.02
VECTOR_RATE = 0.2
WEIGHT_DECAY = 0.1
OUTER_RATE = 0.7
OUTER_MOMENTUM = 0.9


def normalize(source, gain_row, shift_row):
    centre = source - jnp.mean(source, axis=-1, keepdims=True)
    spread = jnp.mean(centre * centre, axis=-1, keepdims=True)
    return centre * lax.rsqrt(spread + EPSILON) * gain_row + shift_row


def gelu_exact(source):
    return jax.nn.gelu(source, approximate=False)


def gelu_slope(source):
    return (
        0.5 * (1.0 + lax.erf(source * 0.7071067811865476))
        + source * jnp.exp(-0.5 * source * source) * 0.3989422804014327
    )


def inner_adamw(master, gradient, moments, step_rate, decay_rate):
    first_moment = 0.9 * moments[0] + 0.1 * gradient
    second_moment = 0.95 * moments[1] + 0.05 * gradient * gradient
    step_ratio = (
        first_moment / (1.0 - 0.9**STEP) / (jnp.sqrt(second_moment / (1.0 - 0.95**STEP)) + 1e-08)
    )
    return (master - step_rate * (step_ratio + decay_rate * master), second_moment)


def outer_nesterov(master, outer_old, difference):
    momentum = OUTER_MOMENTUM * outer_old + difference
    updated = master - OUTER_RATE * (difference + OUTER_MOMENTUM * momentum)
    return (jnp.stack([difference, momentum, updated]), updated.astype(jnp.bfloat16))


def attend_forward(score_scale, operands):
    queries_low, keys_low, values_low = operands
    scores = (
        jnp.einsum("qhe,khe->hqk", queries_low, keys_low, preferred_element_type=jnp.float32)
        * score_scale
    )
    highest = jnp.max(scores, axis=-1, keepdims=True)
    exponent = jnp.exp(scores - highest)
    totals = jnp.sum(exponent, axis=-1, keepdims=True)
    probs_low = (exponent / totals).astype(jnp.bfloat16)
    attended = jnp.einsum("hqk,khe->qhe", probs_low, values_low, preferred_element_type=jnp.float32)
    return (attended.astype(jnp.bfloat16), (highest + jnp.log(totals))[..., 0])


def attend_backward(score_scale, operands):
    queries_low, keys_low, values_low, log_totals, grad_attended = operands
    scores = (
        jnp.einsum("qhe,khe->hqk", queries_low, keys_low, preferred_element_type=jnp.float32)
        * score_scale
    )
    probs_full = jnp.exp(scores - log_totals[..., None])
    grad_probs = jnp.einsum(
        "qhe,khe->hqk", grad_attended, values_low, preferred_element_type=jnp.float32
    )
    grad_values = jnp.einsum(
        "hqk,qhe->khe",
        probs_full.astype(jnp.bfloat16),
        grad_attended,
        preferred_element_type=jnp.float32,
    )
    weighted = jnp.sum(probs_full * grad_probs, axis=-1, keepdims=True)
    grad_scores = (probs_full * (grad_probs - weighted)).astype(jnp.bfloat16)
    grad_queries = (
        jnp.einsum("hqk,khe->qhe", grad_scores, keys_low, preferred_element_type=jnp.float32)
        * score_scale
    )
    grad_keys = (
        jnp.einsum("hqk,qhe->khe", grad_scores, queries_low, preferred_element_type=jnp.float32)
        * score_scale
    )
    return (
        grad_queries.astype(jnp.bfloat16),
        grad_keys.astype(jnp.bfloat16),
        grad_values.astype(jnp.bfloat16),
    )


def local(
    patches,
    output_grad,
    live_counts,
    attn_master,
    mlp_master,
    vector_master,
    attn_moments,
    mlp_moments,
    vector_moments,
    attn_outer,
    mlp_outer,
    vector_outer,
):
    narrow = jnp.bfloat16
    single = jnp.float32
    tensor_index = lax.axis_index("tensor")
    fsdp_index = lax.axis_index("fsdp")
    micro_count = patches.shape[1]
    local_images = patches.shape[2]
    seq_len = patches.shape[3]
    width = patches.shape[4]
    score_scale = HD ** (-0.5)
    tensor_size = lax.axis_size("tensor")

    def whole(master):
        shards = lax.all_gather(master.astype(narrow), ("fsdp", "tensor"), axis=0, tiled=False)
        f_size = lax.axis_size("fsdp")
        shards = shards.reshape((f_size, tensor_size) + master.shape)
        shards = jnp.transpose(shards, (2, 0, 3, 1, 4))
        return shards.reshape(master.shape[0], f_size * master.shape[1], tensor_size * master.shape[2])

    attn_all = whole(attn_master)
    mlp_all = whole(mlp_master)
    owner_counts = jnp.sum(
        jnp.where(jnp.arange(live_counts.shape[2]) == fsdp_index, live_counts[0], 0), axis=-1
    )
    slot_index = tensor_index * local_images + jnp.arange(local_images)
    alive = (slot_index[None, :] < owner_counts[:, None]).astype(single).reshape(-1)[:, None, None]
    image_count = micro_count * local_images
    heads = width // HD
    shape_heads = (image_count, seq_len, heads, HD)
    inputs = patches.reshape(image_count, seq_len, width).astype(single)
    grad_out = alive * output_grad.reshape(image_count, seq_len, width).astype(single)
    grad_two = grad_out.astype(narrow)
    normed_one = normalize(inputs, vector_master[0], vector_master[1]).astype(narrow)

    def dot_in(rows, weight):
        return jnp.einsum("isd,de->ise", rows, weight, preferred_element_type=single)

    def dot_out(rows, weight):
        return jnp.einsum("ise,de->isd", rows, weight, preferred_element_type=single)

    def outer(rows, cols):
        return jnp.einsum("isd,ise->de", rows, cols, preferred_element_type=single).astype(narrow)

    queries_low = (dot_in(normed_one, attn_all[0]) + vector_master[4]).astype(narrow)
    keys_low = dot_in(normed_one, attn_all[1]).astype(narrow)
    values_low = (dot_in(normed_one, attn_all[2]) + vector_master[5]).astype(narrow)
    queries_low = queries_low.reshape(shape_heads)
    keys_low = keys_low.reshape(shape_heads)
    values_low = values_low.reshape(shape_heads)
    attended, log_totals = lax.map(
        partial(attend_forward, score_scale), (queries_low, keys_low, values_low)
    )
    attended = attended.reshape(image_count, seq_len, width)
    resid_one = inputs + dot_out(attended, attn_all[3]) + vector_master[6]
    normed_two = normalize(resid_one, vector_master[2], vector_master[3]).astype(narrow)
    pre_act = dot_in(normed_two, mlp_all[0]) + vector_master[8:].reshape(-1)
    hidden = gelu_exact(pre_act).astype(narrow)
    branch_two = dot_out(hidden, mlp_all[1])
    mixed = (alive * (resid_one + branch_two + vector_master[7])).astype(narrow)
    fc_out = outer(grad_two, hidden)
    grad_pre = (dot_in(grad_two, mlp_all[1]) * gelu_slope(pre_act)).astype(narrow)
    fc_in = outer(normed_two, grad_pre)
    grad_normed_two = dot_out(grad_pre, mlp_all[0])
    unused_two, norm_pull_two = jax.vjp(normalize, resid_one, vector_master[2], vector_master[3])
    back_resid, gain_two, shift_two = norm_pull_two(grad_normed_two)
    grad_resid = grad_out + back_resid
    grad_one = grad_resid.astype(narrow)
    out_grad = outer(grad_one, attended)
    grad_attended = dot_in(grad_one, attn_all[3]).astype(narrow).reshape(shape_heads)
    grad_queries, grad_keys, grad_values = lax.map(
        partial(attend_backward, score_scale),
        (queries_low, keys_low, values_low, log_totals, grad_attended),
    )
    grad_queries = grad_queries.reshape(image_count, seq_len, width)
    grad_keys = grad_keys.reshape(image_count, seq_len, width)
    grad_values = grad_values.reshape(image_count, seq_len, width)
    grad_normed_one = (
        dot_out(grad_queries, attn_all[0])
        + dot_out(grad_keys, attn_all[1])
        + dot_out(grad_values, attn_all[2])
    )
    unused_one, norm_pull_one = jax.vjp(normalize, inputs, vector_master[0], vector_master[1])
    back_inputs, gain_one, shift_one = norm_pull_one(grad_normed_one)
    input_grad = grad_resid + back_inputs

    def owned(whole_grad, shape):
        f_size = lax.axis_size("fsdp")
        parts = whole_grad.reshape(shape[0], f_size, shape[1], tensor_size, shape[2])
        parts = jnp.transpose(parts, (1, 3, 0, 2, 4))
        mine = lax.psum_scatter(parts, "fsdp", scatter_dimension=0, tiled=False)
        return lax.psum_scatter(mine, "tensor", scatter_dimension=0, tiled=False).astype(single)

    mlp_grad = owned(jnp.stack([fc_in, fc_out]), mlp_master.shape)
    attn_grad = owned(
        jnp.stack(
            [
                outer(normed_one, grad_queries),
                outer(normed_one, grad_keys),
                outer(normed_one, grad_values),
                out_grad,
            ]
        ),
        attn_master.shape,
    )

    def total(rows):
        return jnp.sum(rows.astype(single), axis=(0, 1))

    vector_part = jnp.concatenate(
        [
            jnp.stack(
                [
                    gain_one,
                    shift_one,
                    gain_two,
                    shift_two,
                    total(grad_queries),
                    total(grad_values),
                    total(grad_resid),
                    total(grad_out),
                ]
            ),
            total(grad_pre).reshape(-1, width),
        ],
        0,
    )
    vector_grad = lax.psum(vector_part, ("fsdp", "tensor"))
    new_attn, second_attn = inner_adamw(
        attn_master, attn_grad, attn_moments[0], INNER_RATE, WEIGHT_DECAY
    )
    new_mlp, second_mlp = inner_adamw(
        mlp_master, mlp_grad, mlp_moments[0], INNER_RATE, WEIGHT_DECAY
    )
    new_vector, second_vector = inner_adamw(
        vector_master, vector_grad, vector_moments[0], VECTOR_RATE, 0.0
    )
    groups = lax.axis_size("group")

    def group_sum(difference):
        flat = difference.astype(narrow).reshape((groups, -1, difference.shape[-1]))
        mine = lax.psum_scatter(flat, "group", scatter_dimension=0, tiled=False)
        summed = lax.all_gather(mine, "group", axis=0, tiled=False)
        return summed.reshape(difference.shape).astype(single)

    diff_attn = group_sum(attn_master - new_attn)
    diff_mlp = group_sum(mlp_master - new_mlp)
    diff_vector = lax.psum(vector_master - new_vector, "group")
    attn_state, attn_copy = outer_nesterov(attn_master, attn_outer, diff_attn / groups)
    mlp_state, mlp_copy = outer_nesterov(mlp_master, mlp_outer, diff_mlp / groups)
    vector_state, vector_copy = outer_nesterov(vector_master, vector_outer, diff_vector / groups)
    block_output = mixed.reshape(patches.shape)
    patches_grad = input_grad.reshape(patches.shape)
    attn_inner = jnp.stack([attn_grad, second_attn])[None]
    mlp_inner = jnp.stack([mlp_grad, second_mlp])[None]
    vector_inner = jnp.stack([vector_grad, second_vector])[None]
    return (
        block_output,
        patches_grad,
        attn_inner,
        attn_state,
        attn_copy,
        mlp_inner,
        mlp_state,
        mlp_copy,
        vector_inner,
        vector_state,
        vector_copy,
    )


def solution(mesh):
    placed = (
        P("group", None, ("fsdp", "tensor"), None, None),
        P("group", None, ("fsdp", "tensor"), None, None),
        P("group", None, None),
        P(None, "fsdp", "tensor"),
        P(None, "fsdp", "tensor"),
        P(),
        P("group", None, None, "fsdp", "tensor"),
        P("group", None, None, "fsdp", "tensor"),
        P("group", None, None, None),
        P(None, "fsdp", "tensor"),
        P(None, "fsdp", "tensor"),
        P(),
    )
    return jax.shard_map(
        local,
        mesh=mesh,
        in_specs=placed,
        out_specs=(
            P("group", None, ("fsdp", "tensor"), None, None),
            P("group", None, ("fsdp", "tensor"), None, None),
            P("group", None, None, "fsdp", "tensor"),
            P(None, None, "fsdp", "tensor"),
            P(None, "fsdp", "tensor"),
            P("group", None, None, "fsdp", "tensor"),
            P(None, None, "fsdp", "tensor"),
            P(None, "fsdp", "tensor"),
            P("group", None, None, None),
            P(),
            P(),
        ),
        check_vma=False,
    )
```

time: 2530 us -> 1210 us (0.48)
  waiting for transfers between devices: 1790 us -> 343 us
  local copies, waits for them, and re-layouts: 124 us -> 219 us
  matrix products: 322 us -> 353 us
    reduce_scatter x10 -> x4, waiting for transfers between devices: 1140 us -> 245 us  [the longest x2 222 us: owned(): lax.psum_scatter(mine, 'tensor', scatter_dimension=0, tiled=False)]
    all_gather x10 -> x4, waiting for transfers between devices: 566 us -> 78.8 us  [the longest x2 78.8 us: whole(): lax.all_gather(master.astype(narrow), ('fsdp', 'tensor'), axis=0, tiled=F...]
    psum x1 -> x0, waiting for transfers between devices: 79.5 us -> none  [local(): lax.psum((attn_master - new_attn, mlp_master - new_mlp, vector_master - n...]
    another operation x20 -> x18, local copies, waits for them, and re-layouts: 20.1 us -> 80.2 us  [the longest x4 48.5 us: local(): mlp_grad = owned(jnp.stack([fc_in, fc_out]), mlp_master.shape)]
    squeeze x0 -> x6, local copies, waits for them, and re-layouts: none -> 46.5 us  [the longest x1 14.4 us: local(): branch_two = dot_out(hidden, mlp_all[1])]
    convert_element_type x8 -> x2, other arithmetic: 11.5 us -> 43.3 us  [attend_backward(): grad_scores = (probs_full * (grad_probs - weighted)).astype(jnp.bfloat16)]
    reshape x1 -> x3, local copies, waits for them, and re-layouts: 0.01 us -> 29.8 us  [the longest x2 29.8 us: whole(): shards = shards.reshape((f_size, tensor_size) + master.shape)]
    unnamed x189 -> x142, local copies, waits for them, and re-layouts: 50.9 us -> 24.9 us
  transfers between devices with their start and end apart: 21 -> 10, of which waited for: 18 -> 6; matrix products, arithmetic and copies ran while one was open for 21% -> 32% of each run, Pallas kernels for 0% -> 0%
where the time goes in v1:
time: 1210 us; the launch traced here: 1200 us
  matrix products  353 us (29%)
  waiting for transfers between devices  343 us (28%)
  local copies, waits for them, and re-layouts  219 us (18%)
  other arithmetic  217 us (18%)
  blocking collectives  47.3 us (4%)
  between operations  15.4 us (1%)
    reduce_scatter x2, waiting for transfers between devices, owned(): lax.psum_scatter(mine, 'tensor', scatter_dimension=0, tiled=False)  222 us
    all_gather x2, waiting for transfers between devices, whole(): lax.all_gather(master.astype(narrow), ('fsdp', 'tensor'), axis=0, tiled=F...  78.8 us
    dot_general x6, matrix products, dot_in(): jnp.einsum('isd,de->ise', rows, weight, preferred_element_type=single)  73.5 us
    dot_general x6, matrix products, outer(): jnp.einsum('isd,ise->de', rows, cols, preferred_element_type=single)  59.3 us
    dot_general x6, matrix products, dot_out(): jnp.einsum('ise,de->isd', rows, weight, preferred_element_type=single)  55.3 us
    another operation x4, local copies, waits for them, and re-layouts, local(): mlp_grad = owned(jnp.stack([fc_in, fc_out]), mlp_master.shape)  48.5 us
    convert_element_type x1, other arithmetic, local(): hidden = gelu_exact(pre_act).astype(narrow)  46.9 us
    convert_element_type x2, other arithmetic, attend_backward(): grad_scores = (probs_full * (grad_probs - weighted)).astype(jnp.bfloat16)  43.3 us
  transfers between devices with their start and end apart: 10, of which 6 were waited for; matrix products, arithmetic and copies ran while one was open for 32% of the time, Pallas kernels for 0%

profile of v1, /device:TPU:0, one launch (start us, length us, event | category | flops | bytes accessed | tf_op | source)
XLA Modules:
  0.0 1196.0 jit_solution(16260706019813890835)
XLA Ops:
  17.7 77.3 %all-gather.11.cloned.1.call-done = bf16[32,512,256]{2,1,0:T(8,128)(2,1)} async-done(((bf16[4,512,256]{2,1,0:T(8,128)(2,1)}), bf16[32,512,256]{2,1,0:T(8,128)(2,1)}) %all-gather.11.cloned.1.call-update) | async-done | bytes 8388624 | tf_op jit(solution)/shard_map/all_gather | solution.py:126
  160.0 74.3 %while.26 = (s32[]{:T(128)}, bf16[2,577,16,64]{1,3,2,0:T(8,128)(2,1)}, f32[2,16,577]{2,1,0:T(8,128)S(1)}, bf16[2,577,16,64]{1,3,2,0:T(8,128)(2,1)}, bf16[2,577,1...) while((s32[]{:T(128)}, bf16[2,577,16,64]{1,3,2,0:T(8,128)(2,1)}, ...), condition=%wide.region_6.7_spmd, body=%wide.region_3.6_spmd.sunk | while | flops 1412200448 | bytes 97843760 | solution.py:162
  246.7 19.7 %copy.188 = bf16[2,4,2,512,1024]{4,1,3,0,2:T(4,128)(2,1)S(1)} copy(bf16[2,4,2,512,1024]{4,3,2,1,0:T(8,128)(2,1)} %bitcast.364) | data formatting | bytes 33554432 | tf_op jit(solution)/shard_map/reshape | solution.py:128
  275.6 14.4 %reshape.315 = bf16[1024,4096,1]{1,0,2:T(8,128)(2,1)} reshape(bf16[1,2,512,4,1024]{4,3,2,1,0:T(4,128)(2,1)} %get-tuple-element.192) | data formatting | bytes 16777216 | tf_op jit(solution)/shard_map/squeeze | solution.py:170
  304.4 27.9 %fusion.91 = (u8[577,4096]{1,0:T(8,128)(4,1)}, u8[577,4096]{1,0:T(8,128)(4,1)}, f32[2,577,4096]{2,1,0:T(8,128)}) fusion(f32[4096]{0:T(1024)S(1)} %bitcast.379, bf16[1024,4096,1]{1,0,2:T(8,128)(2,1)} %reshape.314, f32[2,577,1024]{2,1,0:T(8,128)} %copy-done.3, f32[1024]{0:T(1024)S(1)} %bitcast.402, f32[1024]{0:T(1024)S(1)} %bitcast.391, ...), kind=kOutput, calls=%fused_computation.139 | convolution fusion | flops 9747810304 | bytes 36783120 | tf_op jit(solution)/shard_map/isd,de->ise/dot_general | solution.py:148
  332.3 22.9 %convert_reduce_fusion = (f32[4096]{0:T(1024)}, bf16[2,577,4096]{2,1,0:T(8,128)(2,1)}) fusion(f32[2,577,4096]{2,1,0:T(8,128)} %get-tuple-element.224, f32[4096]{0:T(1024)S(1)} %bitcast.380, bf16[1024,4096,1]{1,0,2:T(8,128)(2,1)} %reshape.315, f32[2]{0:T(128)S(1)} %copy-done.69, bf16[1,2,1,577,1024]{4,1,3,2,0:T(2,128)(2,1)S(1)} %copy-done.30), kind=kOutput, calls=%fused_computation.74 | convolution fusion | flops 9745442816 | bytes 39145480 | tf_op jit(solution)/shard_map/isd,de->ise/dot_general | solution.py:148
  355.2 17.4 %fusion.156 = (f32[1024]{0:T(1024)}, f32[2,577]{1,0:T(2,128)S(1)}, f32[2,577,1024]{2,1,0:T(8,128)}) fusion(f32[1024]{0:T(1024)S(1)} %bitcast.392, f32[2,577,1024]{2,1,0:T(8,128)S(1)} %bitcast.355, f32[2,577]{1,0:T(2,128)S(1)} %broadcast_multiply_fusion, bf16[2,577,4096]{2,1,0:T(8,128)(2,1)} %get-tuple-element.228, bf16[1024,4096,1]{1,0,2:T(8,128)(2,1)} %reshape.314), kind=kOutput, calls=%fused_computation.239 | convolution fusion | flops 9686360064 | bytes 27313168 | tf_op jit(solution)/shard_map/ise,de->isd/dot_general | solution.py:151
  403.7 163.6 %while.27 = (s32[]{:T(128)}, bf16[2,577,16,64]{1,3,2,0:T(8,128)(2,1)}, bf16[2,577,16,64]{1,3,2,0:T(8,128)(2,1)}, bf16[2,577,16,64]{1,3,2,0:T(8,128)(2,1)}, bf16[...) while((s32[]{:T(128)}, ...), condition=%wide.region_13.14_spmd, body=%wide.region_11.13_spmd.sunk | while | flops 3476060160 | bytes 225671200 | solution.py:182
  430.7 15.8 %multiply_reduce_fusion.8 = (f32[16,577]{1,0:T(8,128)S(1)}, f32[16,577,577]{1,2,0:T(8,128)}) fusion(f32[16,577,577]{1,2,0:T(8,128)} %fusion.219, f32[16,577]{1,0:T(8,128)S(1)} %dynamic-slice_bitcast_fusion.2, bf16[2,577,16,64]{1,3,2,0:T(8,128)(2,1)} %get-tuple-element.380, s32[]{:T(128)S(6)} %copy.210, bf16[2,577,16,64]{1,3,2,0:T(8,128)(2,1)} %get-tuple-element.379), kind=kOutput, calls=%fused_computation.20.clone.1 | convolution fusion | flops 703136768 | bytes 47924416 | tf_op jit(solution)/shard_map/while/body/eval_jaxpr/qhe,khe->hqk/dot_general | solution.py:74
  446.6 21.6 %multiply_convert_fusion.5 = bf16[16,577,577]{1,2,0:T(8,128)(2,1)} fusion(f32[16,577,577]{1,2,0:T(8,128)} %get-tuple-element.329, f32[16,577,577]{1,2,0:T(8,128)} %fusion.219, f32[16,577]{1,0:T(8,128)S(1)} %get-tuple-element.330, f32[16,577]{1,0:T(8,128)S(1)} %dynamic-slice_bitcast_fusion.2), kind=kLoop, calls=%fused_computation.19.clone.1 | loop fusion | flops 26634320 | bytes 53342496 | tf_op jit(solution)/shard_map/while/body/eval_jaxpr/convert_element_type | solution.py:84
  512.2 15.8 %multiply_reduce_fusion.8 = (f32[16,577]{1,0:T(8,128)S(1)}, f32[16,577,577]{1,2,0:T(8,128)}) fusion(f32[16,577,577]{1,2,0:T(8,128)} %fusion.219, f32[16,577]{1,0:T(8,128)S(1)} %dynamic-slice_bitcast_fusion.2, bf16[2,577,16,64]{1,3,2,0:T(8,128)(2,1)} %get-tuple-element.380, s32[]{:T(128)S(6)} %copy.210, bf16[2,577,16,64]{1,3,2,0:T(8,128)(2,1)} %get-tuple-element.379), kind=kOutput, calls=%fused_computation.20.clone.1 | convolution fusion | flops 703136768 | bytes 47924416 | tf_op jit(solution)/shard_map/while/body/eval_jaxpr/qhe,khe->hqk/dot_general | solution.py:74
  528.1 21.6 %multiply_convert_fusion.5 = bf16[16,577,577]{1,2,0:T(8,128)(2,1)} fusion(f32[16,577,577]{1,2,0:T(8,128)} %get-tuple-element.329, f32[16,577,577]{1,2,0:T(8,128)} %fusion.219, f32[16,577]{1,0:T(8,128)S(1)} %get-tuple-element.330, f32[16,577]{1,0:T(8,128)S(1)} %dynamic-slice_bitcast_fusion.2), kind=kLoop, calls=%fused_computation.19.clone.1 | loop fusion | flops 26634320 | bytes 53342496 | tf_op jit(solution)/shard_map/while/body/eval_jaxpr/convert_element_type | solution.py:84
  617.8 46.9 %fusion.57 = bf16[2,577,4096]{2,1,0:T(8,128)(2,1)S(1)} fusion(f32[2,577,4096]{2,1,0:T(8,128)} %get-tuple-element.224, f32[4096]{0:T(1024)S(1)} %bitcast.381, u8[577,4096]{1,0:T(8,128)(4,1)} %get-tuple-element.147, u8[577,4096]{1,0:T(8,128)(4,1)S(1)} %copy-done.29), kind=kLoop, calls=%fused_computation.62 | loop fusion | flops 335601664 | bytes 33103872 | tf_op jit(solution)/shard_map/convert_element_type | solution.py:169
  668.4 15.0 %bitcast_convert_fusion = bf16[1024,4096]{1,0:T(8,128)(2,1)} fusion(bf16[2,577,4096]{2,1,0:T(8,128)(2,1)S(1)} %fusion.57, f32[2]{0:T(128)S(1)} %copy-done.70, bf16[1,2,1,577,1024]{4,1,3,2,0:T(2,128)(2,1)S(1)} %copy-done.31), kind=kOutput, calls=%fused_computation.89 | convolution fusion | flops 9688193024 | bytes 20205576 | tf_op jit(solution)/shard_map/isd,ise->de/dot_general | solution.py:154
  683.4 14.6 %stack.112 = bf16[1,2,512,4,1024]{4,3,2,1,0:T(4,128)(2,1)} reshape(bf16[1024,4096]{1,0:T(8,128)(2,1)} %bitcast_convert_fusion) | data formatting | bytes 16777216 | tf_op jit(solution)/shard_map/stack | solution.py:205
  707.8 18.2 %bitcast_convert_fusion.1 = bf16[1024,4096]{1,0:T(8,128)(2,1)} fusion(bf16[2,577,4096]{2,1,0:T(8,128)(2,1)} %get-tuple-element.228, f32[2,577,1024]{2,1,0:T(8,128)S(1)} %bitcast.357, f32[1024]{0:T(1024)S(1)} %bitcast.403, f32[1024]{0:T(1024)S(1)} %bitcast.395, f32[2,577]{1,0:T(2,128)S(1)} %copy-done.52, f32[2,577]{1,0:T(2,128)S(1)} %copy-done.43), kind=kOutput, calls=%fused_computation.90 | convolution fusion | flops 9690556416 | bytes 22586384 | tf_op jit(solution)/shard_map/isd,ise->de/dot_general | solution.py:154
  726.0 14.6 %stack.111 = bf16[1,2,512,4,1024]{4,3,2,1,0:T(4,128)(2,1)} reshape(bf16[1024,4096]{1,0:T(8,128)(2,1)} %bitcast_convert_fusion.1) | data formatting | bytes 16777216 | tf_op jit(solution)/shard_map/stack | solution.py:205
  764.5 22.8 %reduce-scatter.15.cloned.1.call-done = bf16[1,4,2,512,1024]{4,3,2,1,0:T(8,128)(2,1)} async-done(((bf16[2,4,2,512,1024]{4,3,2,1,0:T(8,128)(2,1)}), bf16[1,4,2,512,1024]{4,3,2,1,0:T(8,128)(2,1)}) %reduce-scatter.15.cloned.1.call-update) | async-done | bytes 8388624 | tf_op jit(solution)/shard_map/reduce_scatter | solution.py:202
  787.4 80.2 %reduce-scatter.13.cloned.1.call-done = bf16[1,4,512,256]{3,2,1,0:T(8,128)(2,1)} async-done(((bf16[4,4,512,256]{3,2,1,0:T(8,128)(2,1)}), bf16[1,4,512,256]{3,2,1,0:T(8,128)(2,1)}) %reduce-scatter.13.cloned.1.call-update) | async-done | bytes 1048592 | tf_op jit(solution)/shard_map/reduce_scatter | solution.py:203
  873.1 141.8 %reduce-scatter.17.cloned.1.call-done = bf16[1,2,512,1024]{3,2,1,0:T(8,128)(2,1)} async-done(((bf16[4,2,512,1024]{3,2,1,0:T(8,128)(2,1)}), bf16[1,2,512,1024]{3,2,1,0:T(8,128)(2,1)}) %reduce-scatter.17.cloned.1.call-update) | async-done | bytes 2097168 | tf_op jit(solution)/shard_map/reduce_scatter | solution.py:203
  1023.1 16.2 %fusion.105 = bf16[1,2,1,577,1024]{4,3,1,2,0:T(8,128)(2,1)S(1)} fusion(f32[2,577,1024]{2,1,0:T(8,128)} %copy-done.3, f32[1024]{0:T(1024)S(1)} %bitcast.400, f32[2]{0:T(128)S(1)} %copy-done.70, bf16[2,577,4096]{2,1,0:T(8,128)(2,1)} %copy-done.19, bf16[1024,4096,1]{1,0,2:T(8,128)(2,1)} %reshape.315), kind=kOutput, calls=%fused_computation.166 | convolution fusion | flops 9685180416 | bytes 24936456 | tf_op jit(solution)/shard_map/ise,de->isd/dot_general | solution.py:151
  1067.0 18.7 %reduce-scatter.21.cloned.1.call-done = bf16[1,256,1024]{2,1,0:T(8,128)(2,1)} async-done(((bf16[4,256,1024]{2,1,0:T(8,128)(2,1)}), bf16[1,256,1024]{2,1,0:T(8,128)(2,1)}) %reduce-scatter.21.cloned.1.call-update) | async-done | bytes 524304
  1098.9 29.3 %psum.14 = f32[12,1024]{1,0:T(8,128)S(1)} all-reduce(f32[12,1024]{1,0:T(8,128)S(1)} %concatenate.5), channel_id=1, replica_groups=mesh['group'=4,'fsdp'=2,'tensor'=4] {'fsdp','tensor'}, use_global_device_ids=true, to_apply=%region_31.32 | all-reduce | flops 12288 | bytes 98304 | tf_op jit(solution)/shard_map/psum | solution.py:239
  1129.1 18.0 %psum.15 = f32[12,1024]{1,0:T(8,128)S(1)} all-reduce(f32[12,1024]{1,0:T(8,128)S(1)} %get-tuple-element.209), channel_id=1, replica_groups=mesh['group'=4,'fsdp'=2,'tensor'=4] {'group'}, use_global_device_ids=true, to_apply=%region_32.33 | all-reduce | flops 12288 | bytes 98304 | tf_op jit(solution)/shard_map/psum | solution.py:259
  (306 shorter events, 489.0 us)
Async XLA Ops:
  7.2 87.8 %all-gather.11.cloned.1.call-start = ((), (), s32[]{:S(2)}) async-start(), calls=%async_computation.12 | async-start | bytes 9437184 | tf_op jit(solution)/shard_map/all_gather | solution.py:126
  9.9 236.8 %all-gather.13.cloned.1.call-start = ((), (), s32[]{:S(2)}) async-start(), calls=%async_computation.13 | async-start | bytes 18874368 | tf_op jit(solution)/shard_map/all_gather | solution.py:126
  14.0 750.0 %reduce-scatter.11.cloned.1.call-start = ((), (), s32[]{:S(2)}) async-start(), calls=%async_computation.6 | async-start | bytes 12582912 | tf_op jit(solution)/shard_map/reduce_scatter | solution.py:202
  16.1 132.7 %copy-start.40 = (f32[2,577]{1,0:T(2,128)}, f32[2,577]{1,0:T(2,128)S(1)}, u32[]{:S(2)}) copy-start(f32[2,577]{1,0:T(2,128)S(1)} %broadcast_multiply_fusion.1) | copy-start | bytes 13852
  17.0 88.1 %copy-start.49 = (f32[2,577]{1,0:T(2,128)}, f32[2,577]{1,0:T(2,128)S(1)}, u32[]{:S(2)}) copy-start(f32[2,577]{1,0:T(2,128)S(1)} %fusion.81) | copy-start | bytes 13852
  17.1 131.7 %copy-start.47 = (f32[2,577]{1,0:T(2,128)}, f32[2,577]{1,0:T(2,128)S(1)}, u32[]{:S(2)}) copy-start(f32[2,577]{1,0:T(2,128)S(1)} %fusion.141) | copy-start | bytes 13852
  17.7 131.1 %copy-start.53 = (f32[1,1024]{1,0:T(1,128)}, f32[1,1024]{1,0:T(1,128)S(1)}, u32[]{:S(2)}) copy-start(f32[1,1024]{1,0:T(1,128)S(1)} %get-tuple-element.221) | copy-start | bytes 12292
  17.7 131.1 %copy-start.65 = (f32[1,1024]{1,0:T(1,128)}, f32[1,1024]{1,0:T(1,128)S(1)}, u32[]{:S(2)}) copy-start(f32[1,1024]{1,0:T(1,128)S(1)} %get-tuple-element.220) | copy-start | bytes 12292
  242.3 135.0 %copy-start.42 = (f32[2,577]{1,0:T(2,128)}, f32[2,577]{1,0:T(2,128)S(1)}, u32[]{:S(2)}) copy-start(f32[2,577]{1,0:T(2,128)S(1)} %broadcast_multiply_fusion) | copy-start | bytes 13852
  245.1 132.1 %copy-start.51 = (f32[2,577]{1,0:T(2,128)}, f32[2,577]{1,0:T(2,128)S(1)}, u32[]{:S(2)}) copy-start(f32[2,577]{1,0:T(2,128)S(1)} %fusion.142) | copy-start | bytes 13852
  403.7 163.6 %copy-start.41 = (f32[2,577]{1,0:T(2,128)S(1)}, f32[2,577]{1,0:T(2,128)}, u32[]{:S(2)}) copy-start(f32[2,577]{1,0:T(2,128)} %copy-done.40) | copy-start | bytes 13852
  403.7 163.6 %copy-start.48 = (f32[2,577]{1,0:T(2,128)S(1)}, f32[2,577]{1,0:T(2,128)}, u32[]{:S(2)}) copy-start(f32[2,577]{1,0:T(2,128)} %copy-done.47) | copy-start | bytes 13852
  403.7 163.6 %copy-start.54 = (f32[1,1024]{1,0:T(1,128)S(1)}, f32[1,1024]{1,0:T(1,128)}, u32[]{:S(2)}) copy-start(f32[1,1024]{1,0:T(1,128)} %copy-done.53) | copy-start | bytes 12292
  403.7 163.6 %copy-start.66 = (f32[1,1024]{1,0:T(1,128)S(1)}, f32[1,1024]{1,0:T(1,128)}, u32[]{:S(2)}) copy-start(f32[1,1024]{1,0:T(1,128)} %copy-done.65) | copy-start | bytes 12292
  616.1 171.2 %reduce-scatter.15.cloned.1.call-start = ((), (), s32[]{:S(2)}) async-start(), calls=%async_computation.9 | async-start | bytes 25165824 | tf_op jit(solution)/shard_map/reduce_scatter | solution.py:202
  763.9 103.7 %reduce-scatter.13.cloned.1.call-start = ((), (), s32[]{:S(2)}) async-start(), calls=%async_computation.7 | async-start | bytes 5242880 | tf_op jit(solution)/shard_map/reduce_scatter | solution.py:203
  764.5 103.1 %copy-start.13 = (f32[4,512,256]{2,1,0:T(8,128)S(1)}, f32[4,512,256]{2,1,0:T(8,128)}, u32[]{:S(2)}) copy-start(f32[4,512,256]{2,1,0:T(8,128)} %param.19) | copy-start | bytes 6291460
  764.5 250.4 %reduce-scatter.17.cloned.1.call-start = ((), (), s32[]{:S(2)}) async-start(), calls=%async_computation.10 | async-start | bytes 10485760 | tf_op jit(solution)/shard_map/reduce_scatter | solution.py:203
  787.3 85.6 %copy-start.39 = (f32[1,2,12,1024]{3,1,2,0:T(2,128)S(1)}, f32[1,2,12,1024]{3,1,2,0:T(2,128)}, u32[]{:S(2)}) copy-start(f32[1,2,12,1024]{3,1,2,0:T(2,128)} %param.24) | copy-start | bytes 294916
  787.4 269.8 %reduce-scatter.19.cloned.1.call-start = ((), (), s32[]{:S(2)}) async-start(), calls=%async_computation.14 | async-start | bytes 1310720
  872.9 212.8 %reduce-scatter.21.cloned.1.call-start = ((), (), s32[]{:S(2)}) async-start(), calls=%async_computation.15 | async-start | bytes 2621440
  873.1 149.9 %copy-start.61 = (f32[1,1024]{1,0:T(1,128)S(1)}, f32[1,1024]{1,0:T(1,128)}, u32[]{:S(2)}) copy-start(f32[1,1024]{1,0:T(1,128)} %get-tuple-element.215) | copy-start | bytes 12292
  1023.0 130.1 %all-gather.7.cloned.1.call-start = ((), (), s32[]{:S(2)}) async-start(), calls=%async_computation.8 | async-start | bytes 1310720 | tf_op jit(solution)/shard_map/all_gather | solution.py:254
  1057.2 110.0 %all-gather.9.cloned.1.call-start = ((), (), s32[]{:S(2)}) async-start(), calls=%async_computation.11 | async-start | bytes 2621440 | tf_op jit(solution)/shard_map/all_gather | solution.py:254
  (71 other events, 941.6 us)
Sparse Core Ops, SparseCore 0:
  10.2 84.7 all-gather.10
  97.1 149.5 all-gather.12
  616.2 14.5 reduce-scatter.10
  764.0 23.2 reduce-scatter.14
  789.5 78.0 reduce-scatter.12
  869.8 145.1 reduce-scatter.16
  1018.4 28.5 reduce-scatter.18
  1050.5 35.1 reduce-scatter.20
  1087.6 26.4 all-gather.6
  1115.8 36.2 all-gather.8
